TPU v7x, 32 devices: a whole 2x2x4 slice. The times are simulated.
32 devices in a mesh: group: 2 (over y), seq: 4 (over z), tensor: 4 (over x, core).
Axes of the slice: x: 2, y: 2, z: 4, core: 2. Of those that a mesh axis runs over, the one named last changes fastest.
Arguments:
- query: bfloat16 [16, 7168], P(('group', 'seq'), 'tensor'), parts along dimension 0, may hold values from -5 to 5
- key_cache: bfloat16 [32, 256, 7168], P(('group', 'seq'), None, 'tensor'), parts along dimension 0, may hold values from -5 to 5
- value_cache: bfloat16 [32, 256, 7168], P(('group', 'seq'), None, 'tensor'), parts along dimension 0, may hold values from -6 to 6
- alibi_slopes: float32 [56], P('tensor'), may hold values from 0 to 1, as said below
- block_seq: int32 [32], P(('group', 'seq')), parts along dimension 0, may hold values from 0 to 7, as said below
- block_pos: int32 [32], P(('group', 'seq')), parts along dimension 0, may hold values from 0 to 2, as said below
- lengths: int32 [16], P('group'), parts along dimension 0, may hold values from 1 to 768, as said below
- out_weight: bfloat16 [7168, 14336], P('tensor', 'seq'), may hold values from -0.5 to 0.5
Outputs:
- mixed: bfloat16 [16, 14336], P(('group', 'tensor'), 'seq'), parts along dimension 0
There are 2 independent parts, one for each index of `group`. A program takes and returns all parts, laid end to end along the dimension named above; an argument that names none is the same for every part. Nothing has to cross between parts.
Inputs may be any that keep to these rules, and one draw needn't show every extreme that they name: `block_seq`: every sequence owns at least one block and at most 3; the blocks of sequence s have block_pos 0 to n_s - 1, each once. block_pos of a block is below the number of blocks its sequence owns. `lengths`: A sequence that owns n blocks has a length above 256 * (n - 1) and at most 256 * n. `alibi_slopes`: positive slopes.
All inputs are finite; a program needn't handle non-finite values.
Results may differ from a plain program's by a relative error of at most 0.0054.
Values may be sent and summed in bfloat16 or wider, within the bound.
No kernel may reach another device: no remote copies, remote signals or barrier semaphores. Data moves between devices by JAX's collectives and lax.ppermute only.
A program may use at most 64 MiB of HBM per device.

v0:
```python
import math
import jax
import jax.numpy as jnp
from jax import lax
from jax.sharding import PartitionSpec as P


def local(query, key_cache, value_cache, alibi_slopes, block_seq, block_pos, lengths, out_weight):
    heads = alibi_slopes.shape[0]
    features = query.shape[1]
    head_size = features // heads
    blocks_here = key_cache.shape[0]
    block_len = key_cache.shape[1]
    seq_count = lengths.shape[0]
    scale = 1.0 / math.sqrt(head_size)
    whole_query = lax.all_gather(query, "seq", axis=0, tiled=True)
    query_rows = jnp.take(whole_query, block_seq, axis=0).reshape(blocks_here, heads, head_size)
    keys = key_cache.reshape(blocks_here, block_len, heads, head_size)
    values = value_cache.reshape(blocks_here, block_len, heads, head_size)
    scores = (
        jnp.einsum("bthd,bhd->bht", keys, query_rows, preferred_element_type=jnp.float32) * scale
    )
    owner_length = lengths[block_seq]
    placed = block_pos[:, None] * block_len + jnp.arange(block_len, dtype=jnp.int32)[None, :]
    live = (placed < owner_length[:, None])[:, None, :]
    distance = (owner_length[:, None] - 1 - placed).astype(jnp.float32)
    scores = scores - alibi_slopes[None, :, None] * distance[:, None, :]
    scores = jnp.where(live, scores, -1e30)
    block_top = jnp.max(scores, axis=2)
    weights = jnp.where(live, jnp.exp(scores - block_top[:, :, None]), 0.0)
    block_total = jnp.sum(weights, axis=2)
    block_acc = jnp.einsum(
        "bht,bthd->bhd", weights.astype(jnp.bfloat16), values, preferred_element_type=jnp.float32
    )
    seq_ids = jnp.arange(seq_count, dtype=jnp.int32)
    owned = (block_seq[None, :] == seq_ids[:, None])[:, :, None]
    local_top = jnp.max(jnp.where(owned, block_top[None], -1e30), axis=1)
    factor = jnp.where(owned, jnp.exp(block_top[None] - local_top[:, None, :]), 0.0)
    local_total = jnp.sum(factor * block_total[None], axis=1)
    local_acc = jnp.einsum("sbh,bhd->shd", factor, block_acc, precision=lax.Precision.HIGHEST)
    tops, totals, accs = (
        lax.all_to_all(local_top[None], "seq", split_axis=1, concat_axis=0, tiled=True),
        lax.all_to_all(local_total[None], "seq", split_axis=1, concat_axis=0, tiled=True),
        lax.all_to_all(local_acc[None], "seq", split_axis=1, concat_axis=0, tiled=True),
    )
    best = jnp.max(tops, axis=0)
    scaling = jnp.exp(tops - best[None])
    home_total = jnp.sum(totals * scaling, axis=0)
    home_acc = jnp.sum(accs * scaling[..., None], axis=0)
    mine = (
        (home_acc / home_total[:, :, None])
        .astype(jnp.bfloat16)
        .reshape(home_acc.shape[0], features)
    )
    attention = lax.all_gather(mine, "seq", axis=0, tiled=True)
    mixed = lax.psum_scatter(
        jnp.dot(attention, out_weight, preferred_element_type=jnp.float32),
        "tensor",
        scatter_dimension=0,
        tiled=True,
    )
    return mixed.astype(jnp.bfloat16)


def solution(mesh):
    placed = (
        P(("group", "seq"), "tensor"),
        P(("group", "seq"), None, "tensor"),
        P(("group", "seq"), None, "tensor"),
        P("tensor"),
        P(("group", "seq")),
        P(("group", "seq")),
        P("group"),
        P("tensor", "seq"),
    )
    return jax.shard_map(
        local, mesh=mesh, in_specs=placed, out_specs=P(("group", "tensor"), "seq"), check_vma=False
    )
```

profile of v0, /device:TPU:0, one launch (start us, length us, event | category | flops | bytes accessed | tf_op | source)
XLA Modules:
  0.0 95.4 jit_solution(14486349411866468453)
XLA Ops:
  0.0 0.0 copy-start
  0.0 0.7 compare_select_fusion
  0.7 0.7 compare_and_fusion
  1.3 0.7 iota_compare_fusion
  2.1 0.0 copy-done
  2.1 0.6 gather_fusion
  2.7 0.7 broadcast_add_fusion
  3.4 0.1 fusion.16
  3.5 0.1 subtract_convert_fusion
  3.5 15.1 %all-gather = bf16[4,2,1792]{2,1,0:T(2,128)(2,1)S(1)} all-gather(bf16[1,2,1792]{2,1,0:T(2,128)(2,1)} %bitcast.41), channel_id=1, replica_groups=mesh['group'=2,'seq'=4,'tensor'=4] {'seq'}, dimensions={0}, use_global_device_ids=true | all-gather | bytes 35840 | tf_op jit(solution)/shard_map/all_gather | solution.py:16
  18.6 0.6 gather_fusion.1
  19.2 6.0 %copy.49 = bf16[4,256,1792]{1,2,0:T(8,128)(2,1)} copy(bf16[4,256,1792]{2,1,0:T(8,128)(2,1)} %param.9) | data formatting | bytes 7340032 | tf_op args[1]
  25.2 0.0 copy-start.1
  25.2 0.1 select_bitcast_fusion
  25.3 2.6 %fusion.9 = f32[4,14,1,256]{3,2,1,0:T(1,128)S(1)} fusion(bf16[4,256,14,128]{1,3,2,0:T(8,128)(2,1)} %bitcast.33, bf16[4,14,128,1]{2,1,0,3:T(8,128)(2,1)S(1)} %select_bitcast_fusion), kind=kOutput, calls=%fused_computation.16 | convolution fusion | flops 3670016 | bytes 3741696 | tf_op jit(solution)/shard_map/bthd,bhd->bht/dot_general | solution.py:21
  27.9 0.0 copy-done.1
  27.9 0.2 fusion.18
  28.0 0.1 select_reduce_fusion
  28.1 0.7 copy.54
  28.8 4.7 %all-to-all-start.1 = ((f32[1,8,14]{2,0,1:T(1,128)}), f32[1,8,14]{2,0,1:T(1,128)S(1)}, u32[]{:S(2)}, u32[]{:S(2)}) async-start(f32[1,8,14]{2,0,1:T(1,128)} %copy.54), calls=%async_computation.1 | async-start | bytes 8192 | tf_op jit(solution)/shard_map/all_to_all | solution.py:42
  33.6 0.2 fusion.4
  33.7 0.1 multiply_reduce_fusion.1
  33.8 6.0 %copy.50 = bf16[4,256,1792]{1,2,0:T(8,128)(2,1)} copy(bf16[4,256,1792]{2,1,0:T(8,128)(2,1)} %param.10) | data formatting | bytes 7340032 | tf_op args[2]
  39.8 0.0 copy-start.2
  39.8 3.1 %fusion.2 = f32[4,14,1,128]{3,2,1,0:T(1,128)S(1)} fusion(bf16[4,256,14,128]{1,3,2,0:T(8,128)(2,1)} %bitcast.34, bf16[4,14,256,1]{2,0,1,3:T(4,128)(2,1)S(1)} %get-tuple-element.10), kind=kOutput, calls=%fused_computation.6 | convolution fusion | flops 3670016 | bytes 3727360 | tf_op jit(solution)/shard_map/bht,bthd->bhd/dot_general | solution.py:32
  42.9 0.4 convolution_bitcast_fusion
  43.3 0.7 copy.57
  44.0 0.0 all-to-all-done.1
  44.0 5.1 %all-to-all-start.2 = ((f32[1,8,14]{2,0,1:T(1,128)}), f32[1,8,14]{2,0,1:T(1,128)S(1)}, u32[]{:S(2)}, u32[]{:S(2)}) async-start(f32[1,8,14]{2,0,1:T(1,128)} %copy.57), calls=%async_computation.2 | async-start | bytes 8192 | tf_op jit(solution)/shard_map/all_to_all | solution.py:43
  49.1 0.7 copy.51
  49.7 0.0 copy-done.2
  49.7 0.6 dynamic-slice
  51.0 3.7 %all-to-all-done.2 = f32[1,8,14]{2,0,1:T(1,128)S(1)} async-done(((f32[1,8,14]{2,0,1:T(1,128)}), f32[1,8,14]{2,0,1:T(1,128)S(1)}, u32[]{:S(2)}, u32[]{:S(2)}) %all-to-all-start.2) | async-done | bytes 480 | tf_op jit(solution)/shard_map/all_to_all | solution.py:43
  54.6 3.3 %all-to-all-start = ((f32[1,8,14,128]{3,0,2,1:T(1,128)}), f32[1,8,14,128]{3,0,2,1:T(1,128)S(1)}, u32[]{:S(2)}, u32[]{:S(2)}) async-start(f32[1,8,14,128]{3,0,2,1:T(1,128)} %copy.51), calls=%async_computation | async-start | bytes 114688 | tf_op jit(solution)/shard_map/all_to_all | solution.py:44
  58.0 0.1 copy.55
  58.1 0.1 copy.58
  58.2 5.5 %all-to-all-done = f32[1,8,14,128]{3,0,2,1:T(1,128)S(1)} async-done(((f32[1,8,14,128]{3,0,2,1:T(1,128)}), f32[1,8,14,128]{3,0,2,1:T(1,128)S(1)}, u32[]{:S(2)}, u32[]{:S(2)}) %all-to-all-start) | async-done | bytes 57376 | tf_op jit(solution)/shard_map/all_to_all | solution.py:44
  63.6 0.1 multiply_reduce_fusion
  63.8 0.1 fusion.15
  63.9 13.2 %all-gather.1 = bf16[4,2,1792]{2,1,0:T(2,128)(2,1)S(1)} all-gather(bf16[1,2,1792]{2,1,0:T(2,128)(2,1)S(1)} %fusion.15), channel_id=1, replica_groups=mesh['group'=2,'seq'=4,'tensor'=4] {'seq'}, dimensions={0}, use_global_device_ids=true | all-gather | bytes 35840 | tf_op jit(solution)/shard_map/all_gather | solution.py:55
  77.1 6.4 %fusion.20 = f32[8,3584]{1,0:T(8,128)S(1)} fusion(bf16[8,1792]{1,0:T(8,128)(2,1)S(1)} %reshape.152, bf16[1792,3584]{1,0:T(8,128)(2,1)} %param.15), kind=kOutput, calls=%fused_computation.41 | convolution fusion | flops 102760448 | bytes 12988416 | tf_op jit(solution)/shard_map/dot_general | solution.py:57
  83.5 11.3 %all-reduce = bf16[8,3584]{1,0:T(8,128)(2,1)S(1)} all-reduce(f32[8,3584]{1,0:T(8,128)S(1)} %fusion.20), channel_id=2, replica_groups=mesh['group'=2,'seq'=4,'tensor'=4] {'tensor'}, use_global_device_ids=true, to_apply=%region_7.8.clone | all-reduce | flops 28672 | bytes 172032
  94.7 0.6 dynamic-slice_convert_fusion
  (7 shorter events, 0.1 us)
Async XLA Ops:
  0.0 2.1 %copy-start = (s32[8]{0:T(128)S(1)}, s32[8]{0:T(128)}, u32[]{:S(2)}) copy-start(s32[8]{0:T(128)} %param.14) | copy-start | bytes 100
  25.2 2.7 %copy-start.1 = (f32[14]{0:T(128)S(1)}, f32[14]{0:T(128)}, u32[]{:S(2)}) copy-start(f32[14]{0:T(128)} %param.11) | copy-start | bytes 172
  28.8 15.2 %all-to-all-start.1 = ((f32[1,8,14]{2,0,1:T(1,128)}), f32[1,8,14]{2,0,1:T(1,128)S(1)}, u32[]{:S(2)}, u32[]{:S(2)}) async-start(f32[1,8,14]{2,0,1:T(1,128)} %copy.54), calls=%async_computation.1 | async-start | bytes 8192 | tf_op jit(solution)/shard_map/all_to_all | solution.py:42
  39.8 9.9 %copy-start.2 = (u32[32]{0:T(128)S(1)}, u32[32]{0:T(128)}, u32[]{:S(2)}) copy-start(u32[32]{0:T(128)} %constant.39) | copy-start | bytes 388
  44.0 10.7 %all-to-all-start.2 = ((f32[1,8,14]{2,0,1:T(1,128)}), f32[1,8,14]{2,0,1:T(1,128)S(1)}, u32[]{:S(2)}, u32[]{:S(2)}) async-start(f32[1,8,14]{2,0,1:T(1,128)} %copy.57), calls=%async_computation.2 | async-start | bytes 8192 | tf_op jit(solution)/shard_map/all_to_all | solution.py:43
  54.6 9.0 %all-to-all-start = ((f32[1,8,14,128]{3,0,2,1:T(1,128)}), f32[1,8,14,128]{3,0,2,1:T(1,128)S(1)}, u32[]{:S(2)}, u32[]{:S(2)}) async-start(f32[1,8,14,128]{3,0,2,1:T(1,128)} %copy.51), calls=%async_computation | async-start | bytes 114688 | tf_op jit(solution)/shard_map/all_to_all | solution.py:44
where the time goes:
time: 96.1 us; the launch traced here: 95.4 us
  blocking collectives  39.5 us (41%)
  local copies, waits for them, and re-layouts  16.7 us (17%)
  starting transfers between devices  13.1 us (14%)
  matrix products  12.5 us (13%)
  waiting for transfers between devices  9.12 us (9%)
  other arithmetic  3.75 us (4%)
    all_gather x1, blocking collectives, local(): whole_query = lax.all_gather(query, 'seq', axis=0, tiled=True)  15.1 us
    all_gather x1, blocking collectives, local(): attention = lax.all_gather(mine, 'seq', axis=0, tiled=True)  13.2 us
    unnamed x11, local copies, waits for them, and re-layouts  12.6 us
    unnamed x1, blocking collectives  11.3 us
    dot_general x1, matrix products, local(): jnp.dot(attention, out_weight, preferred_element_type=jnp.float32)  6.41 us
    all_to_all x1, waiting for transfers between devices, local(): lax.all_to_all(local_acc[None], 'seq', split_axis=1, concat_axis=0, tiled...  5.46 us
    all_to_all x1, starting transfers between devices, local(): lax.all_to_all(local_total[None], 'seq', split_axis=1, concat_axis=0, til...  5.09 us
    all_to_all x1, starting transfers between devices, local(): lax.all_to_all(local_top[None], 'seq', split_axis=1, concat_axis=0, tiled...  4.74 us
  transfers between devices with their start and end apart: 3, of which 2 were waited for; matrix products, arithmetic and copies ran while one was open for 13% of the time, Pallas kernels for 0%

commit v1 on v0

--- a/solution.py
+++ b/solution.py
@@ -52,7 +52,14 @@
         .astype(jnp.bfloat16)
         .reshape(home_acc.shape[0], features)
     )
-    attention = lax.all_gather(mine, "seq", axis=0, tiled=True)
+    ways, here = (lax.axis_size("seq"), lax.axis_index("seq"))
+    attention, reach = (mine, 1)
+    while reach < ways:
+        theirs = lax.ppermute(attention, "seq", [(d, d ^ reach) for d in range(ways)])
+        mine_first = jnp.concatenate([attention, theirs], axis=0)
+        theirs_first = jnp.concatenate([theirs, attention], axis=0)
+        attention = jnp.where(here & reach == 0, mine_first, theirs_first)
+        reach = 2 * reach
     mixed = lax.psum_scatter(
         jnp.dot(attention, out_weight, preferred_element_type=jnp.float32),
         "tensor",

time: 96.1 us -> 90.9 us (0.946)
  blocking collectives: 39.5 us -> 26.3 us
  waiting for transfers between devices: 9.12 us -> 15.3 us
  starting transfers between devices: 13.1 us -> 14.9 us
    all_gather x1 -> x0, blocking collectives: 13.2 us -> none  [local(): attention = lax.all_gather(mine, 'seq', axis=0, tiled=True)]
    ppermute x0 -> x2, waiting for transfers between devices: none -> 5.32 us  [local(): lax.ppermute(attention, 'seq', [(d, d ^ reach) for d in range(ways)])]
    ppermute x0 -> x2, starting transfers between devices: none -> 1.82 us  [local(): lax.ppermute(attention, 'seq', [(d, d ^ reach) for d in range(ways)])]
    unnamed x11 -> x10, local copies, waits for them, and re-layouts: 12.6 us -> 12.5 us
  transfers between devices with their start and end apart: 3 -> 5, of which waited for: 2 -> 4; matrix products, arithmetic and copies ran while one was open for 13% -> 13% of each run, Pallas kernels for 0% -> 0%
where the time goes in v1:
time: 90.9 us; the launch traced here: 90.2 us
  blocking collectives  26.3 us (29%)
  local copies, waits for them, and re-layouts  16.6 us (18%)
  waiting for transfers between devices  15.3 us (17%)
  starting transfers between devices  14.9 us (16%)
  matrix products  12.5 us (14%)
  other arithmetic  3.8 us (4%)
    all_gather x1, blocking collectives, local(): whole_query = lax.all_gather(query, 'seq', axis=0, tiled=True)  15.1 us
    unnamed x10, local copies, waits for them, and re-layouts  12.5 us
    unnamed x1, blocking collectives  11.3 us
    dot_general x1, matrix products, local(): jnp.dot(attention, out_weight, preferred_element_type=jnp.float32)  6.4 us
    all_to_all x1, waiting for transfers between devices, local(): lax.all_to_all(local_acc[None], 'seq', split_axis=1, concat_axis=0, tiled...  5.46 us
    ppermute x2, waiting for transfers between devices, local(): lax.ppermute(attention, 'seq', [(d, d ^ reach) for d in range(ways)])  5.32 us
    all_to_all x1, starting transfers between devices, local(): lax.all_to_all(local_total[None], 'seq', split_axis=1, concat_axis=0, til...  5.09 us
    all_to_all x1, starting transfers between devices, local(): lax.all_to_all(local_top[None], 'seq', split_axis=1, concat_axis=0, tiled...  4.74 us
  transfers between devices with their start and end apart: 5, of which 4 were waited for; matrix products, arithmetic and copies ran while one was open for 13% of the time, Pallas kernels for 0%

profile of v1, /device:TPU:0, one launch (start us, length us, event | category | flops | bytes accessed | tf_op | source)
XLA Modules:
  0.0 90.2 jit_solution(6438257981220577048)
XLA Ops:
  0.0 0.0 copy-start
  0.0 0.7 compare_select_fusion
  0.7 0.7 compare_and_fusion
  1.3 0.7 iota_compare_fusion
  2.1 0.0 copy-done
  2.1 0.6 gather_fusion
  2.7 0.7 broadcast_add_fusion
  3.4 0.1 fusion.23
  3.5 0.1 subtract_convert_fusion
  3.5 15.1 %all-gather = bf16[4,2,1792]{2,1,0:T(2,128)(2,1)S(1)} all-gather(bf16[1,2,1792]{2,1,0:T(2,128)(2,1)} %bitcast.40), channel_id=1, replica_groups=mesh['group'=2,'seq'=4,'tensor'=4] {'seq'}, dimensions={0}, use_global_device_ids=true | all-gather | bytes 35840 | tf_op jit(solution)/shard_map/all_gather | solution.py:16
  18.6 0.6 gather_fusion.1
  19.2 6.0 %copy.49 = bf16[4,256,1792]{1,2,0:T(8,128)(2,1)} copy(bf16[4,256,1792]{2,1,0:T(8,128)(2,1)} %param.9) | data formatting | bytes 7340032 | tf_op args[1]
  25.2 0.0 copy-start.1
  25.2 0.1 select_bitcast_fusion
  25.2 2.6 %fusion.15 = f32[4,14,1,256]{3,2,1,0:T(1,128)S(1)} fusion(bf16[4,256,14,128]{1,3,2,0:T(8,128)(2,1)} %bitcast.32, bf16[4,14,128,1]{2,1,0,3:T(8,128)(2,1)S(1)} %select_bitcast_fusion), kind=kOutput, calls=%fused_computation.23 | convolution fusion | flops 3670016 | bytes 3741696 | tf_op jit(solution)/shard_map/bthd,bhd->bht/dot_general | solution.py:21
  27.9 0.0 copy-done.1
  27.9 0.2 fusion.26
  28.0 0.1 select_reduce_fusion
  28.1 0.7 copy.54
  28.8 4.7 %all-to-all-start.1 = ((f32[1,8,14]{2,0,1:T(1,128)}), f32[1,8,14]{2,0,1:T(1,128)S(1)}, u32[]{:S(2)}, u32[]{:S(2)}) async-start(f32[1,8,14]{2,0,1:T(1,128)} %copy.54), calls=%async_computation.1 | async-start | bytes 8192 | tf_op jit(solution)/shard_map/all_to_all | solution.py:42
  33.6 0.2 fusion.4
  33.7 6.0 %copy.50 = bf16[4,256,1792]{1,2,0:T(8,128)(2,1)} copy(bf16[4,256,1792]{2,1,0:T(8,128)(2,1)} %param.10) | data formatting | bytes 7340032 | tf_op args[2]
  39.7 0.0 copy-start.2
  39.7 3.1 %fusion.2 = f32[4,14,1,128]{3,2,1,0:T(1,128)S(1)} fusion(bf16[4,256,14,128]{1,3,2,0:T(8,128)(2,1)} %bitcast.33, bf16[4,14,256,1]{2,0,1,3:T(4,128)(2,1)S(1)} %get-tuple-element.10), kind=kOutput, calls=%fused_computation.6 | convolution fusion | flops 3670016 | bytes 3727360 | tf_op jit(solution)/shard_map/bht,bthd->bhd/dot_general | solution.py:32
  42.8 0.1 multiply_reduce_fusion.1
  42.9 0.7 copy.57
  43.6 0.0 all-to-all-done.1
  43.6 5.1 %all-to-all-start.2 = ((f32[1,8,14]{2,0,1:T(1,128)}), f32[1,8,14]{2,0,1:T(1,128)S(1)}, u32[]{:S(2)}, u32[]{:S(2)}) async-start(f32[1,8,14]{2,0,1:T(1,128)} %copy.57), calls=%async_computation.2 | async-start | bytes 8192 | tf_op jit(solution)/shard_map/all_to_all | solution.py:43
  48.7 0.4 convolution_bitcast_fusion
  49.1 0.7 copy.51
  49.8 4.5 %all-to-all-done.2 = f32[1,8,14]{2,0,1:T(1,128)S(1)} async-done(((f32[1,8,14]{2,0,1:T(1,128)}), f32[1,8,14]{2,0,1:T(1,128)S(1)}, u32[]{:S(2)}, u32[]{:S(2)}) %all-to-all-start.2) | async-done | bytes 480 | tf_op jit(solution)/shard_map/all_to_all | solution.py:43
  54.3 3.3 %all-to-all-start = ((f32[1,8,14,128]{3,0,2,1:T(1,128)}), f32[1,8,14,128]{3,0,2,1:T(1,128)S(1)}, u32[]{:S(2)}, u32[]{:S(2)}) async-start(f32[1,8,14,128]{3,0,2,1:T(1,128)} %copy.51), calls=%async_computation | async-start | bytes 114688 | tf_op jit(solution)/shard_map/all_to_all | solution.py:44
  57.6 0.1 copy.55
  57.7 0.1 copy.58
  57.8 5.5 %all-to-all-done = f32[1,8,14,128]{3,0,2,1:T(1,128)S(1)} async-done(((f32[1,8,14,128]{3,0,2,1:T(1,128)}), f32[1,8,14,128]{3,0,2,1:T(1,128)S(1)}, u32[]{:S(2)}, u32[]{:S(2)}) %all-to-all-start) | async-done | bytes 57376 | tf_op jit(solution)/shard_map/all_to_all | solution.py:44
  63.2 0.1 multiply_reduce_fusion
  63.4 0.1 fusion.22
  63.5 1.0 %collective-permute-start = (bf16[2,1792]{1,0:T(2,128)(2,1)S(1)}, bf16[2,1792]{1,0:T(2,128)(2,1)S(1)}, u32[]{:S(2)}, u32[]{:S(2)}) collective-permute-start(bf16[2,1792]{1,0:T(2,128)(2,1)S(1)} %fusion.22), channel_id=1, source_target_pairs={{0,4},{4,0},{8,12},{12,8},{1,5},{5,1},{9,13},{13,9},{2,6},{6,2},{1... | collective-permute-start | bytes 21512 | tf_op jit(solution)/shard_map/ppermute | solution.py:58
  64.5 2.7 %collective-permute-done = bf16[2,1792]{1,0:T(2,128)(2,1)S(1)} collective-permute-done((bf16[2,1792]{1,0:T(2,128)(2,1)S(1)}, bf16[2,1792]{1,0:T(2,128)(2,1)S(1)}, u32[]{:S(2)}, u32[]{:S(2)}) %collective-permute-start) | collective-permute-done | bytes 7200 | tf_op jit(solution)/shard_map/ppermute | solution.py:58
  67.2 0.8 collective-permute-start.1
  68.0 0.0 copy-done.2
  68.0 0.6 dynamic-slice
  69.2 2.7 %collective-permute-done.1 = bf16[4,1792]{1,0:T(4,128)(2,1)S(1)} collective-permute-done((bf16[4,1792]{1,0:T(4,128)(2,1)S(1)}, bf16[4,1792]{1,0:T(4,128)(2,1)S(1)}, u32[]{:S(2)}, u32[]{:S(2)}) %collective-permute-start.1) | collective-permute-done | bytes 14368 | tf_op jit(solution)/shard_map/ppermute | solution.py:58
  71.9 6.4 %fusion.7 = f32[8,3584]{1,0:T(8,128)S(1)} fusion(bf16[1792,3584]{1,0:T(8,128)(2,1)} %param.15, bf16[4,1792]{1,0:T(4,128)(2,1)S(1)} %collective-permute-done.1, bf16[4,1792]{1,0:T(4,128)(2,1)S(1)} %maximum_select_fusion.2, pred[]{:T(512)S(6)} %eq.23), kind=kOutput, calls=%fused_computation.14 | convolution fusion | flops 102889472 | bytes 12988417 | tf_op jit(solution)/shard_map/dot_general | solution.py:64
  78.3 11.3 %all-reduce = bf16[8,3584]{1,0:T(8,128)(2,1)S(1)} all-reduce(f32[8,3584]{1,0:T(8,128)S(1)} %fusion.7), channel_id=2, replica_groups=mesh['group'=2,'seq'=4,'tensor'=4] {'tensor'}, use_global_device_ids=true, to_apply=%region_7.8.clone | all-reduce | flops 28672 | bytes 172032
  89.6 0.6 dynamic-slice_convert_fusion
  (7 shorter events, 0.1 us)
Async XLA Ops:
  0.0 2.1 %copy-start = (s32[8]{0:T(128)S(1)}, s32[8]{0:T(128)}, u32[]{:S(2)}) copy-start(s32[8]{0:T(128)} %param.14) | copy-start | bytes 100
  25.2 2.7 %copy-start.1 = (f32[14]{0:T(128)S(1)}, f32[14]{0:T(128)}, u32[]{:S(2)}) copy-start(f32[14]{0:T(128)} %param.11) | copy-start | bytes 172
  28.8 14.8 %all-to-all-start.1 = ((f32[1,8,14]{2,0,1:T(1,128)}), f32[1,8,14]{2,0,1:T(1,128)S(1)}, u32[]{:S(2)}, u32[]{:S(2)}) async-start(f32[1,8,14]{2,0,1:T(1,128)} %copy.54), calls=%async_computation.1 | async-start | bytes 8192 | tf_op jit(solution)/shard_map/all_to_all | solution.py:42
  39.7 28.3 %copy-start.2 = (u32[32]{0:T(128)S(1)}, u32[32]{0:T(128)}, u32[]{:S(2)}) copy-start(u32[32]{0:T(128)} %constant.49) | copy-start | bytes 388
  43.6 10.7 %all-to-all-start.2 = ((f32[1,8,14]{2,0,1:T(1,128)}), f32[1,8,14]{2,0,1:T(1,128)S(1)}, u32[]{:S(2)}, u32[]{:S(2)}) async-start(f32[1,8,14]{2,0,1:T(1,128)} %copy.57), calls=%async_computation.2 | async-start | bytes 8192 | tf_op jit(solution)/shard_map/all_to_all | solution.py:43
  54.3 9.0 %all-to-all-start = ((f32[1,8,14,128]{3,0,2,1:T(1,128)}), f32[1,8,14,128]{3,0,2,1:T(1,128)S(1)}, u32[]{:S(2)}, u32[]{:S(2)}) async-start(f32[1,8,14,128]{3,0,2,1:T(1,128)} %copy.51), calls=%async_computation | async-start | bytes 114688 | tf_op jit(solution)/shard_map/all_to_all | solution.py:44
  63.5 3.7 %collective-permute-start = (bf16[2,1792]{1,0:T(2,128)(2,1)S(1)}, bf16[2,1792]{1,0:T(2,128)(2,1)S(1)}, u32[]{:S(2)}, u32[]{:S(2)}) collective-permute-start(bf16[2,1792]{1,0:T(2,128)(2,1)S(1)} %fusion.22), channel_id=1, source_target_pairs={{0,4},{4,0},{8,12},{12,8},{1,5},{5,1},{9,13},{13,9},{2,6},{6,2},{1... | collective-permute-start | bytes 21512 | tf_op jit(solution)/shard_map/ppermute | solution.py:58
  67.2 4.7 %collective-permute-start.1 = (bf16[4,1792]{1,0:T(4,128)(2,1)S(1)}, bf16[4,1792]{1,0:T(4,128)(2,1)S(1)}, u32[]{:S(2)}, u32[]{:S(2)}) collective-permute-start(bf16[4,1792]{1,0:T(4,128)(2,1)S(1)} %maximum_select_fusion.2), channel_id=1, source_target_pairs={{0,8},{4,12},{8,0},{12,4},{1,9},{5,13},{9,1},{13,5},{2,10},{6,14},... | collective-permute-start | bytes 43016 | tf_op jit(solution)/shard_map/ppermute | solution.py:58
